TPU v7x, 32 devices: a whole 2x2x4 slice. The times are simulated.
32 devices in a mesh: row: 8 (over z, x), col: 4 (over y, core).
Axes of the slice: x: 2, y: 2, z: 4, core: 2. Of those that a mesh axis runs over, the one named last changes fastest.
Arguments:
- basis_blocks: float32 [8, 16, 262144], P(None, None, ('col', 'row')), may hold values from -6 to 6
- tile_values: bfloat16 [4, 8, 384, 128, 128], P('col', 'row'), may hold values from -0.375 to 0.375
- tile_rows: int32 [4, 8, 384], P('col', 'row'), may hold values from 0 to 511
- tile_column: int32 [4, 8, 384], P('col', 'row'), may hold values from 0 to 255
- tile_count: int32 [4, 8], P('col', 'row'), may hold values from 1 to 384, as said below
- diagonal: float32 [262144], P(('col', 'row')), may hold values from 1 to 6
Outputs:
- new_block: float32 [16, 262144], P(None, ('col', 'row'))
- coefficients: float32 [8, 16, 16], replicated
- triangle: float32 [16, 16], replicated
Inputs may be any that keep to these rules, and one draw needn't show every extreme that they name: Each operator block stores tile_count tiles in its first slots; at most 384, and some block has exactly 384 in every draw. Slots past the count hold arbitrary data and are ignored.
All inputs are finite; a program needn't handle non-finite values.
Results may differ from a plain program's by a relative error of at most 0.0031.
Values may be sent and summed in bfloat16 or wider, within the bound.
A program may use at most 128 MiB of HBM per device.

v0:
```python
import jax
import jax.numpy as jnp
from jax import lax
from jax.sharding import PartitionSpec as P


def local(basis_blocks, tile_values, tile_rows, tile_column, tile_count, diagonal):
    rhs_width = basis_blocks.shape[1]
    seg_rows = basis_blocks.shape[2]
    total_rows = seg_rows * lax.axis_size("row") * lax.axis_size("col")
    block_tiles = lax.axis_size("row") * seg_rows // 128
    vector = basis_blocks[-1].astype(jnp.bfloat16)
    expanded = lax.all_gather(vector, "col", axis=1, tiled=True)
    xblocks = expanded.reshape(rhs_width, -1, 128)
    values = tile_values[0, 0]
    row_ids = tile_rows[0, 0]
    column_ids = tile_column[0, 0]
    live_count = tile_count[0, 0]
    live_tiles = jnp.arange(values.shape[0], dtype=jnp.int32) < live_count
    gathered = jnp.take(xblocks, column_ids, axis=1)
    products = jnp.einsum("stj,tji->tsi", gathered, values, preferred_element_type=jnp.float32)
    inside = live_tiles & (row_ids >= 0) & (row_ids < 0 + block_tiles)
    segment_ids = jnp.where(inside, row_ids - 0, block_tiles)
    summed = jax.ops.segment_sum(products, segment_ids, num_segments=block_tiles + 1)
    folded = lax.psum_scatter(summed[:block_tiles], "row", scatter_dimension=0, tiled=True)
    image_rows = folded.transpose(1, 0, 2).reshape(rhs_width, seg_rows)
    image_rows = image_rows + diagonal[None, :] * basis_blocks[-1]
    highest = lax.Precision.HIGHEST
    local_proj = jnp.einsum("kap,bp->kab", basis_blocks, image_rows, precision=highest)
    local_self = jnp.dot(image_rows, image_rows.T, precision=highest)
    local_basis = jnp.einsum("kap,lcp->kalc", basis_blocks, basis_blocks, precision=highest)
    proj_sum, image_sum, basis_sum = lax.psum((local_proj, local_self, local_basis), ("row", "col"))
    coefficients = proj_sum / total_rows
    image_gram = image_sum / total_rows
    basis_gram = basis_sum / total_rows
    projected = image_rows - jnp.einsum(
        "kab,kap->bp", coefficients, basis_blocks, precision=highest
    )
    cross_term = jnp.einsum("kab,kad->bd", coefficients, coefficients, precision=highest)
    basis_term = jnp.einsum(
        "kab,kalc,lcd->bd", coefficients, basis_gram, coefficients, precision=highest
    )
    gram_matrix = image_gram - 2.0 * cross_term + basis_term
    lower_factor = jnp.linalg.cholesky(gram_matrix)
    new_block = lax.linalg.triangular_solve(lower_factor, projected, left_side=True, lower=True)
    return (new_block, coefficients, lower_factor.T)


def solution(mesh):
    in_specs = (
        P(None, None, ("col", "row")),
        P("col", "row", None, None, None),
        P("col", "row", None),
        P("col", "row", None),
        P("col", "row"),
        P(("col", "row")),
    )
    out_specs = (P(None, ("col", "row")), P(), P())
    return jax.shard_map(local, mesh=mesh, in_specs=in_specs, out_specs=out_specs, check_vma=False)
```

profile of v0, /device:TPU:0, one launch (start us, length us, event | category | flops | bytes accessed | tf_op | source)
XLA Modules:
  0.0 285.5 jit_solution(4340497072909810050)
XLA Ops:
  8.0 1.8 bitcast_convert_fusion
  10.5 0.7 reduce.7
  11.2 0.7 fusion.22
  11.9 0.7 fusion.23
  12.7 17.7 %all-gather.2.cloned.1.call-done = bf16[16,32768]{1,0:T(8,128)(2,1)} async-done(((bf16[16,8192]{1,0:T(8,128)(2,1)}), bf16[16,32768]{1,0:T(8,128)(2,1)}) %all-gather.2.cloned.1.call-update) | async-done | bytes 1048592 | tf_op jit(solution)/shard_map/all_gather | solution.py:13
  30.4 1.4 copy_bitcast_fusion
  31.8 2.6 gather_fusion
  34.4 6.9 %fusion = f32[384,16,128]{2,1,0:T(8,128)S(1)} fusion(bf16[1,1,384,128,128]{4,3,2,1,0:T(8,128)(2,1)} %param.7, bf16[384,16,128]{2,1,0:T(8,128)(2,1)} %gather_fusion, pred[384]{0:T(512)(128)(4,1)S(1)} %compare_and_fusion), kind=kOutput, calls=%fused_computation.2 | convolution fusion | flops 202113024 | bytes 17301888 | tf_op jit(solution)/shard_map/stj,tji->tsi/dot_general | solution.py:21
  41.2 2.2 broadcast_in_dim.19
  43.5 51.1 %scatter_fusion = f32[513,16,128]{2,1,0:T(8,128)} fusion(f32[513,16,128]{2,1,0:T(8,128)} %broadcast_in_dim.19, s32[384]{0:T(512)S(1)} %fusion.23, f32[384,16,128]{2,1,0:T(8,128)S(1)} %fusion), kind=kCustom, calls=%fused_computation.1 | custom fusion | flops 786432 | bytes 9438720 | tf_op jit(solution)/shard_map/scatter-add | solution.py:24
  94.6 4.4 %slice.21 = f32[512,16,128]{2,1,0:T(8,128)} slice(f32[513,16,128]{2,1,0:T(8,128)} %scatter_fusion), slice={[0:512], [0:16], [0:128]} | slice | bytes 8388608 | tf_op jit(solution)/shard_map/slice | solution.py:25
  99.3 18.0 %fusion.3 = f32[8,16,8,16]{3,1,2,0:T(8,128)} fusion(f32[8,16,8192]{2,1,0:T(8,128)} %param.6), kind=kOutput, calls=%fused_computation.6 | convolution fusion | flops 1610612736 | bytes 4259840 | tf_op jit(solution)/shard_map/kap,lcp->kalc/dot_general | solution.py:31
  117.3 1.1 slice_bitcast_fusion
  118.5 70.4 %reduce-scatter.2.cloned.1.call-done = f32[64,16,128]{2,1,0:T(8,128)} async-done(((f32[512,16,128]{2,1,0:T(8,128)}), f32[64,16,128]{2,1,0:T(8,128)}) %reduce-scatter.2.cloned.1.call-update) | async-done | bytes 524304 | tf_op jit(solution)/shard_map/reduce_scatter | solution.py:25
  188.9 17.2 %convolution_bitcast_fusion.1 = f32[8,16,16]{1,2,0:T(8,128)S(1)} fusion(f32[8,16,8192]{2,1,0:T(8,128)} %param.6, f32[8192]{0:T(1024)S(1)} %copy-done.1, f32[64,16,128]{2,1,0:T(8,128)} %reduce-scatter.2.cloned.1.call-done), kind=kOutput, calls=%fused_computation.12 | convolution fusion | flops 201588736 | bytes 5283840 | tf_op jit(solution)/shard_map/kap,bp->kab/dot_general | solution.py:29
  206.1 1.0 convolution_bitcast_fusion.5
  207.1 41.0 %all-reduce = (f32[8,16,16]{1,2,0:T(8,128)S(1)}, f32[16,16]{0,1:T(8,128)S(1)}) all-reduce(f32[8,16,16]{1,2,0:T(8,128)S(1)} %convolution_bitcast_fusion.1, f32[16,16]{0,1:T(8,128)S(1)} %convolution_bitcast_fusion.5), channel_id=1, replica_groups=mesh['row'=8,'col'=4] {'row','col'}, use_global_device_ids=true, to_apply=%region_3.4 | all-reduce | flops 2304 | bytes 18432 | tf_op jit(solution)/shard_map/psum | solution.py:32
  248.1 14.4 %all-reduce.3.cloned.1.call-done = f32[8,16,8,16]{3,1,2,0:T(8,128)} async-done(((f32[8,16,8,16]{3,1,2,0:T(8,128)}), f32[8,16,8,16]{3,1,2,0:T(8,128)}) %all-reduce.3.cloned.1.call-update) | async-done | bytes 65552 | tf_op jit(solution)/shard_map/psum | solution.py:32
  262.5 1.4 convolution_bitcast_fusion.2
  264.4 1.5 cholesky.16
  267.2 1.2 custom-call.6
  269.1 0.7 copy.41
  269.9 6.7 %fusion.2 = f32[16,8192]{1,0:T(8,128)S(1)} fusion(f32[8,16,8192]{2,1,0:T(8,128)} %param.6, f32[8192]{0:T(1024)S(1)} %copy-done.1, f32[8,16,16]{1,2,0:T(8,128)S(1)} %get-tuple-element.12, f32[64,16,128]{2,1,0:T(8,128)S(1)} %copy-done), kind=kOutput, calls=%fused_computation.5 | convolution fusion | flops 201721856 | bytes 5808128 | tf_op jit(solution)/shard_map/kab,kap->bp/dot_general | solution.py:36
  276.6 1.4 fusion.18
  (22 shorter events, 3.0 us)
Async XLA Ops:
  8.0 22.4 %all-gather.2.cloned.1.call-start = ((), (), s32[]{:S(2)}) async-start(), calls=%async_computation.1 | async-start | bytes 1310720 | tf_op jit(solution)/shard_map/all_gather | solution.py:13
  9.8 179.0 %reduce-scatter.2.cloned.1.call-start = ((), (), s32[]{:S(2)}) async-start(), calls=%async_computation.2 | async-start | bytes 4718592 | tf_op jit(solution)/shard_map/reduce_scatter | solution.py:25
  99.0 89.8 %copy-start.1 = (f32[8192]{0:T(1024)S(1)}, f32[8192]{0:T(1024)}, u32[]{:S(2)}) copy-start(f32[8192]{0:T(1024)} %param.11) | copy-start | bytes 98308
  99.0 163.4 %all-reduce.3.cloned.1.call-start = ((), (), s32[]{:S(2)}) async-start(), calls=%async_computation.3 | async-start | bytes 1048576 | tf_op jit(solution)/shard_map/psum | solution.py:32
  188.9 17.2 %copy-start = (f32[64,16,128]{2,1,0:T(8,128)S(1)}, f32[64,16,128]{2,1,0:T(8,128)}, u32[]{:S(2)}) copy-start(f32[64,16,128]{2,1,0:T(8,128)} %reduce-scatter.2.cloned.1.call-done) | copy-start | bytes 1572868
Sparse Core Ops, SparseCore 0:
  10.9 19.4 all-gather.1
  99.1 89.6 reduce-scatter.1
Sparse Core Ops, SparseCore 1:
  117.4 145.0 all-reduce.2
where the time goes:
time: 288 us; the launch traced here: 285 us
  waiting for transfers between devices  103 us (36%)
  other arithmetic  57.3 us (20%)
  matrix products  53.1 us (18%)
  blocking collectives  41 us (14%)
  between operations  16.2 us (6%)
  local copies, waits for them, and re-layouts  15.1 us (5%)
    reduce_scatter x1, waiting for transfers between devices, local(): lax.psum_scatter(summed[:block_tiles], 'row', scatter_dimension=0, tiled=...  70.4 us
    scatter-add x1, other arithmetic, local(): jax.ops.segment_sum(products, segment_ids, num_segments=block_tiles + 1)  51.1 us
    psum x1, blocking collectives, local(): lax.psum((local_proj, local_self, local_basis), ('row', 'col'))  41 us
    dot_general x1, matrix products, local(): jnp.einsum('kap,lcp->kalc', basis_blocks, basis_blocks, precision=highest)  18 us
    all_gather x1, waiting for transfers between devices, local(): expanded = lax.all_gather(vector, 'col', axis=1, tiled=True)  17.7 us
    dot_general x1, matrix products, local(): jnp.einsum('kap,bp->kab', basis_blocks, image_rows, precision=highest)  17.2 us
    psum x1, waiting for transfers between devices, local(): lax.psum((local_proj, local_self, local_basis), ('row', 'col'))  14.4 us
    dot_general x1, matrix products, local(): jnp.einsum('stj,tji->tsi', gathered, values, preferred_element_type=jnp.f...  6.87 us
  transfers between devices with their start and end apart: 3, of which 3 were waited for; matrix products, arithmetic and copies ran while one was open for 14% of the time, Pallas kernels for 0%

commit v1 on v0

--- a/solution.py
+++ b/solution.py
@@ -10,7 +10,10 @@
     total_rows = seg_rows * lax.axis_size("row") * lax.axis_size("col")
     block_tiles = lax.axis_size("row") * seg_rows // 128
     vector = basis_blocks[-1].astype(jnp.bfloat16)
-    expanded = lax.all_gather(vector, "col", axis=1, tiled=True)
+    peers = lax.axis_size("col")
+    shards = jnp.stack([vector for _ in range(peers)])
+    shards = lax.all_to_all(shards, "col", split_axis=0, concat_axis=0)
+    expanded = jnp.concatenate(shards, axis=1)
     xblocks = expanded.reshape(rhs_width, -1, 128)
     values = tile_values[0, 0]
     row_ids = tile_rows[0, 0]

time: 288 us -> 288 us (level)
  waiting for transfers between devices: 103 us -> 97.1 us
  starting transfers between devices: 0.31 us -> 4.49 us
    all_gather x1 -> x0, waiting for transfers between devices: 17.7 us -> none  [local(): expanded = lax.all_gather(vector, 'col', axis=1, tiled=True)]
    all_to_all x0 -> x1, waiting for transfers between devices: none -> 11.7 us  [local(): shards = lax.all_to_all(shards, 'col', split_axis=0, concat_axis=0)]
    all_to_all x0 -> x1, starting transfers between devices: none -> 4.26 us  [local(): shards = lax.all_to_all(shards, 'col', split_axis=0, concat_axis=0)]
    another operation x0 -> x4, local copies, waits for them, and re-layouts: none -> 3.93 us  [the longest x2 2.13 us: local(): shards = jnp.stack([vector for _ in range(peers)])]
where the time goes in v1:
time: 288 us; the launch traced here: 286 us
  waiting for transfers between devices  97.1 us (34%)
  other arithmetic  57.3 us (20%)
  matrix products  53.1 us (18%)
  blocking collectives  40.9 us (14%)
  local copies, waits for them, and re-layouts  16.6 us (6%)
  between operations  16.2 us (6%)
  starting transfers between devices  4.49 us (2%)
    reduce_scatter x1, waiting for transfers between devices, local(): lax.psum_scatter(summed[:block_tiles], 'row', scatter_dimension=0, tiled=...  71 us
    scatter-add x1, other arithmetic, local(): jax.ops.segment_sum(products, segment_ids, num_segments=block_tiles + 1)  51.1 us
    psum x1, blocking collectives, local(): lax.psum((local_proj, local_self, local_basis), ('row', 'col'))  40.9 us
    dot_general x1, matrix products, local(): jnp.einsum('kap,lcp->kalc', basis_blocks, basis_blocks, precision=highest)  18 us
    dot_general x1, matrix products, local(): jnp.einsum('kap,bp->kab', basis_blocks, image_rows, precision=highest)  17.2 us
    psum x1, waiting for transfers between devices, local(): lax.psum((local_proj, local_self, local_basis), ('row', 'col'))  14.4 us
    all_to_all x1, waiting for transfers between devices, local(): shards = lax.all_to_all(shards, 'col', split_axis=0, concat_axis=0)  11.7 us
    dot_general x1, matrix products, local(): jnp.einsum('stj,tji->tsi', gathered, values, preferred_element_type=jnp.f...  6.87 us
  transfers between devices with their start and end apart: 3, of which 3 were waited for; matrix products, arithmetic and copies ran while one was open for 14% of the time, Pallas kernels for 0%

profile of v1, /device:TPU:0, one launch (start us, length us, event | category | flops | bytes accessed | tf_op | source)
XLA Modules:
  0.0 285.7 jit_solution(3299121353029831825)
XLA Ops:
  8.0 1.1 fusion.15
  9.1 1.1 stack.10
  10.1 4.3 %all-to-all-start = ((bf16[4,16,8192]{2,1,0:T(8,128)(2,1)}), bf16[4,16,8192]{2,1,0:T(8,128)(2,1)S(1)}, u32[]{:S(2)}, u32[]{:S(2)}) async-start(bf16[4,16,8192]{2,1,0:T(8,128)(2,1)} %stack.10), calls=%async_computation | async-start | bytes 2097152 | tf_op jit(solution)/shard_map/all_to_all | solution.py:15
  17.2 11.7 %all-to-all-done = bf16[4,16,8192]{2,1,0:T(8,128)(2,1)S(1)} async-done(((bf16[4,16,8192]{2,1,0:T(8,128)(2,1)}), bf16[4,16,8192]{2,1,0:T(8,128)(2,1)S(1)}, u32[]{:S(2)}, u32[]{:S(2)}) %all-to-all-start) | async-done | bytes 1048608 | tf_op jit(solution)/shard_map/all_to_all | solution.py:15
  28.8 0.8 copy.30
  29.6 1.1 reshape_reshape.3
  31.5 2.6 gather_fusion
  34.0 6.9 %fusion = f32[384,16,128]{2,1,0:T(8,128)S(1)} fusion(bf16[1,1,384,128,128]{4,3,2,1,0:T(8,128)(2,1)} %param.7, bf16[384,16,128]{2,1,0:T(8,128)(2,1)} %gather_fusion, pred[384]{0:T(512)(128)(4,1)S(1)} %compare_and_fusion), kind=kOutput, calls=%fused_computation.2 | convolution fusion | flops 202113024 | bytes 17301888 | tf_op jit(solution)/shard_map/stj,tji->tsi/dot_general | solution.py:24
  40.9 2.2 broadcast_in_dim.19
  43.1 51.1 %scatter_fusion = f32[513,16,128]{2,1,0:T(8,128)} fusion(f32[513,16,128]{2,1,0:T(8,128)} %broadcast_in_dim.19, s32[384]{0:T(512)S(1)} %fusion.24, f32[384,16,128]{2,1,0:T(8,128)S(1)} %fusion), kind=kCustom, calls=%fused_computation.1 | custom fusion | flops 786432 | bytes 9438720 | tf_op jit(solution)/shard_map/scatter-add | solution.py:27
  94.2 4.4 %slice.21 = f32[512,16,128]{2,1,0:T(8,128)} slice(f32[513,16,128]{2,1,0:T(8,128)} %scatter_fusion), slice={[0:512], [0:16], [0:128]} | slice | bytes 8388608 | tf_op jit(solution)/shard_map/slice | solution.py:28
  98.9 18.0 %fusion.3 = f32[8,16,8,16]{3,1,2,0:T(8,128)} fusion(f32[8,16,8192]{2,1,0:T(8,128)} %param.6), kind=kOutput, calls=%fused_computation.6 | convolution fusion | flops 1610612736 | bytes 4259840 | tf_op jit(solution)/shard_map/kap,lcp->kalc/dot_general | solution.py:34
  116.9 1.1 slice_bitcast_fusion
  118.2 71.0 %reduce-scatter.2.cloned.1.call-done = f32[64,16,128]{2,1,0:T(8,128)} async-done(((f32[512,16,128]{2,1,0:T(8,128)}), f32[64,16,128]{2,1,0:T(8,128)}) %reduce-scatter.2.cloned.1.call-update) | async-done | bytes 524304 | tf_op jit(solution)/shard_map/reduce_scatter | solution.py:28
  189.1 17.2 %convolution_bitcast_fusion.1 = f32[8,16,16]{1,2,0:T(8,128)S(1)} fusion(f32[8,16,8192]{2,1,0:T(8,128)} %param.6, f32[8192]{0:T(1024)S(1)} %copy-done.1, f32[64,16,128]{2,1,0:T(8,128)} %reduce-scatter.2.cloned.1.call-done), kind=kOutput, calls=%fused_computation.12 | convolution fusion | flops 201588736 | bytes 5283840 | tf_op jit(solution)/shard_map/kap,bp->kab/dot_general | solution.py:32
  206.4 1.0 convolution_bitcast_fusion.5
  207.4 40.9 %all-reduce = (f32[8,16,16]{1,2,0:T(8,128)S(1)}, f32[16,16]{0,1:T(8,128)S(1)}) all-reduce(f32[8,16,16]{1,2,0:T(8,128)S(1)} %convolution_bitcast_fusion.1, f32[16,16]{0,1:T(8,128)S(1)} %convolution_bitcast_fusion.5), channel_id=1, replica_groups=mesh['row'=8,'col'=4] {'row','col'}, use_global_device_ids=true, to_apply=%region_3.4 | all-reduce | flops 2304 | bytes 18432 | tf_op jit(solution)/shard_map/psum | solution.py:35
  248.3 14.4 %all-reduce.3.cloned.1.call-done = f32[8,16,8,16]{3,1,2,0:T(8,128)} async-done(((f32[8,16,8,16]{3,1,2,0:T(8,128)}), f32[8,16,8,16]{3,1,2,0:T(8,128)}) %all-reduce.3.cloned.1.call-update) | async-done | bytes 65552 | tf_op jit(solution)/shard_map/psum | solution.py:35
  262.7 1.4 convolution_bitcast_fusion.2
  264.7 1.5 cholesky.16
  267.5 1.2 custom-call.6
  269.4 0.7 copy.43
  270.1 6.7 %fusion.2 = f32[16,8192]{1,0:T(8,128)S(1)} fusion(f32[8,16,8192]{2,1,0:T(8,128)} %param.6, f32[8192]{0:T(1024)S(1)} %copy-done.1, f32[8,16,16]{1,2,0:T(8,128)S(1)} %get-tuple-element.12, f32[64,16,128]{2,1,0:T(8,128)S(1)} %copy-done), kind=kOutput, calls=%fused_computation.5 | convolution fusion | flops 201721856 | bytes 5808128 | tf_op jit(solution)/shard_map/kab,kap->bp/dot_general | solution.py:39
  276.9 1.4 fusion.19
  (24 shorter events, 5.7 us)
Async XLA Ops:
  10.1 18.7 %all-to-all-start = ((bf16[4,16,8192]{2,1,0:T(8,128)(2,1)}), bf16[4,16,8192]{2,1,0:T(8,128)(2,1)S(1)}, u32[]{:S(2)}, u32[]{:S(2)}) async-start(bf16[4,16,8192]{2,1,0:T(8,128)(2,1)} %stack.10), calls=%async_computation | async-start | bytes 2097152 | tf_op jit(solution)/shard_map/all_to_all | solution.py:15
  14.4 174.7 %reduce-scatter.2.cloned.1.call-start = ((), (), s32[]{:S(2)}) async-start(), calls=%async_computation.2 | async-start | bytes 4718592 | tf_op jit(solution)/shard_map/reduce_scatter | solution.py:28
  98.7 90.4 %copy-start.1 = (f32[8192]{0:T(1024)S(1)}, f32[8192]{0:T(1024)}, u32[]{:S(2)}) copy-start(f32[8192]{0:T(1024)} %param.11) | copy-start | bytes 98308
  98.7 164.1 %all-reduce.3.cloned.1.call-start = ((), (), s32[]{:S(2)}) async-start(), calls=%async_computation.3 | async-start | bytes 1048576 | tf_op jit(solution)/shard_map/psum | solution.py:35
  189.1 17.2 %copy-start = (f32[64,16,128]{2,1,0:T(8,128)S(1)}, f32[64,16,128]{2,1,0:T(8,128)}, u32[]{:S(2)}) copy-start(f32[64,16,128]{2,1,0:T(8,128)} %reduce-scatter.2.cloned.1.call-done) | copy-start | bytes 1572868
Sparse Core Ops, SparseCore 0:
  98.8 90.2 reduce-scatter.1
Sparse Core Ops, SparseCore 1:
  117.0 145.7 all-reduce.2
